TPU v7x, 32 devices: a whole 2x2x4 slice. The times are simulated.
32 devices in a mesh: sx: 8 (over z, y), sy: 4 (over x, core).
Axes of the slice: x: 2, y: 2, z: 4, core: 2. Of those that a mesh axis runs over, the one named last changes fastest.
Arguments:
- tensors: bfloat16 [2, 8, 4, 1024, 256], P(None, 'sx', 'sy'), may hold values from -6 to 6
- gates: bfloat16 [5, 2, 2, 256, 256], replicated, may hold values from -0.1875 to 0.1875
- closing_rows: bfloat16 [2, 4096, 1024], P(None, ('sx', 'sy')), may hold values from -0.125 to 0.125
- closing_columns: float32 [2, 4096, 256], P(None, ('sx', 'sy')), may hold values from -0.25 to 0.25
Outputs:
- amplitudes: float32 [2, 4096], replicated
All inputs are finite; a program needn't handle non-finite values.
Results may differ from a plain program's by a relative error of at most 0.012.
Values may be sent and summed in bfloat16 or wider, within the bound.
A program may use at most 64 MiB of HBM per device.

v0:
```python
import jax
import jax.numpy as jnp
from jax import lax
from jax.sharding import PartitionSpec as P


def mixing_matrix(gate_pair, sign):
    own_top = jnp.concatenate([gate_pair[0, 0], gate_pair[0, 1]], axis=1)
    own_low = jnp.concatenate([-gate_pair[0, 1], gate_pair[0, 0]], axis=1)
    far_top = jnp.concatenate([gate_pair[1, 0], gate_pair[1, 1]], axis=1) * sign
    far_low = jnp.concatenate([-gate_pair[1, 1], gate_pair[1, 0]], axis=1) * sign
    return jnp.concatenate([own_top, own_low, far_top, far_low], axis=0)


def combine(own, partner, matrix):
    width = own.shape[-1]
    leading = own.shape[1:-1]
    joined = jnp.concatenate([own[0], own[1], partner[0], partner[1]], axis=-1).reshape(
        -1, 4 * width
    )
    result = jnp.dot(joined, matrix, preferred_element_type=jnp.float32).astype(jnp.bfloat16)
    real_part = result[:, :width].reshape(leading + (width,))
    imag_part = result[:, width:].reshape(leading + (width,))
    return jnp.stack([real_part, imag_part])


def local_section(grouped, gate_pair, axis_dim, bit_pos):
    shape = grouped.shape
    count = shape[axis_dim]
    split = shape[:axis_dim] + (count >> bit_pos + 1, 2, 1 << bit_pos) + shape[axis_dim + 1 :]
    blocks = grouped.reshape(split)
    lower = lax.index_in_dim(blocks, 0, axis_dim + 1, keepdims=False)
    upper = lax.index_in_dim(blocks, 1, axis_dim + 1, keepdims=False)
    new_lower = combine(lower, upper, mixing_matrix(gate_pair, 1.0))
    new_upper = combine(upper, lower, mixing_matrix(gate_pair, -1.0))
    return jnp.stack([new_lower, new_upper], axis=axis_dim + 1).reshape(shape)


def close_columns(projected, closing_columns):
    amp_real = jnp.sum(
        projected[0] * closing_columns[0] - projected[1] * closing_columns[1], axis=-1
    )
    amp_imag = jnp.sum(
        projected[0] * closing_columns[1] + projected[1] * closing_columns[0], axis=-1
    )
    return jnp.stack([amp_real, amp_imag])


def combine_rows(closing_rows, current):
    proj_real = jnp.dot(closing_rows[0], current[0], preferred_element_type=jnp.float32) - jnp.dot(
        closing_rows[1], current[1], preferred_element_type=jnp.float32
    )
    proj_imag = jnp.dot(closing_rows[0], current[1], preferred_element_type=jnp.float32) + jnp.dot(
        closing_rows[1], current[0], preferred_element_type=jnp.float32
    )
    return jnp.stack([proj_real, proj_imag])


def local(tensors, gates, closing_rows, closing_columns):
    current = tensors[:, 0, 0]
    rows_dev = current.shape[1]
    width = current.shape[2]
    count_x = lax.axis_size("sx")
    count_y = lax.axis_size("sy")
    bits_x = count_x.bit_length() - 1
    bits_y = count_y.bit_length() - 1
    grouped = lax.all_to_all(
        current.reshape(2, count_x, rows_dev // count_x, width),
        "sx",
        split_axis=1,
        concat_axis=1,
        tiled=True,
    )
    for bit_pos in range(bits_x):
        grouped = local_section(grouped, gates[bit_pos], 1, bit_pos)
    current = lax.all_to_all(grouped, "sx", split_axis=1, concat_axis=1, tiled=True).reshape(
        2, rows_dev, width
    )
    grouped = lax.all_to_all(
        current.reshape(2, count_y, rows_dev // count_y, width),
        "sy",
        split_axis=1,
        concat_axis=1,
        tiled=True,
    )
    for bit_pos in range(bits_y):
        grouped = local_section(grouped, gates[bits_x + bit_pos], 1, bit_pos)
    current = lax.all_to_all(grouped, "sy", split_axis=1, concat_axis=1, tiled=True).reshape(
        2, rows_dev, width
    )
    closed = close_columns(combine_rows(closing_rows, current), closing_columns)
    return lax.all_gather(closed, ("sx", "sy"), axis=1, tiled=True)


def solution(mesh):
    placed = (
        P(None, "sx", "sy", None, None),
        P(),
        P(None, ("sx", "sy"), None),
        P(None, ("sx", "sy"), None),
    )
    return jax.shard_map(local, mesh=mesh, in_specs=placed, out_specs=P(), check_vma=False)
```

profile of v0, /device:TPU:0, one launch (start us, length us, event | category | flops | bytes accessed | tf_op | source)
XLA Modules:
  0.0 157.4 jit_solution(10815839486201930402)
XLA Ops:
  0.0 2.3 %copy.47 = bf16[2,8,128,256]{3,2,0,1:T(8,128)(2,1)} copy(bf16[2,8,128,256]{3,2,1,0:T(8,128)(2,1)} %bitcast.207) | data formatting | bytes 2097152 | tf_op jit(solution)/shard_map/reshape;squeeze | solution.py:68
  2.3 7.3 %all-to-all-start = ((bf16[2,8,128,256]{3,2,0,1:T(8,128)(2,1)}), bf16[2,8,128,256]{3,2,0,1:T(8,128)(2,1)S(1)}, u32[]{:S(2)}, u32[]{:S(2)}) async-start(bf16[2,8,128,256]{3,2,0,1:T(8,128)(2,1)} %copy.47), calls=%async_computation | async-start | bytes 2097152 | tf_op jit(solution)/shard_map/all_to_all | solution.py:67
  9.6 1.9 %slice_bitcast_fusion = (bf16[2,2,256,256]{3,2,1,0:T(8,128)(2,1)S(1)}, bf16[2,2,256,256]{3,2,1,0:T(8,128)(2,1)S(1)}, bf16[2,2,256,256]{3,2,1,0:T(8,128)(2,1)S(1)...) fusion(bf16[5,2,2,256,256]{4,3,2,1,0:T(8,128)(2,1)} %param.5), kind=kLoop, calls=%fused_computation.162 | loop fusion | bytes 5242880 | tf_op jit(solution)/shard_map/squeeze | solution.py:87
  11.5 0.7 slice_bitcast_fusion.23
  12.2 0.7 fusion.156
  13.0 0.9 maximum_multiply_fusion
  13.9 0.8 slice_bitcast_fusion.15
  14.7 0.9 maximum_multiply_fusion.2
  15.6 0.8 fusion.160
  16.3 0.9 maximum_multiply_fusion.4
  17.2 18.2 %all-to-all-done = bf16[2,8,128,256]{3,2,0,1:T(8,128)(2,1)S(1)} async-done(((bf16[2,8,128,256]{3,2,0,1:T(8,128)(2,1)}), bf16[2,8,128,256]{3,2,0,1:T(8,128)(2,1)S(1)}, u32[]{:S(2)}, u32[]{:S(2)}) %all-to-all-start) | async-done | bytes 1048608 | tf_op jit(solution)/shard_map/all_to_all | solution.py:67
  35.4 0.1 fusion.171
  35.5 0.8 copy-done.23
  36.4 0.7 convolution_convert_fusion.9
  37.2 0.2 copy-done.5
  37.4 0.1 copy-done.6
  37.5 0.7 convolution_convert_fusion.8
  38.3 0.1 maximum_maximum_fusion.1
  38.4 0.1 fusion.170
  38.6 0.7 copy-done.11
  39.4 0.7 convolution_convert_fusion.7
  40.1 0.2 copy-done.3
  40.4 0.1 copy-done.4
  40.4 0.7 convolution_convert_fusion.6
  41.4 0.1 pad_maximum_fusion
  41.5 0.1 fusion.169
  41.6 0.7 copy-done.10
  42.3 0.7 convolution_convert_fusion.5
  43.0 0.2 copy-done.1
  43.3 0.1 copy-done.2
  43.4 0.7 convolution_convert_fusion.4
  44.3 0.1 pad_maximum_fusion.1
  44.4 0.1 copy.56
  44.5 29.3 %all_to_all.20 = bf16[2,8,128,256]{3,2,0,1:T(8,128)(2,1)S(1)} all-to-all(bf16[2,8,128,256]{3,2,0,1:T(8,128)(2,1)S(1)} %copy.56), channel_id=1, replica_groups=mesh['sx'=8,'sy'=4] {'sx'}, dimensions={1} | all-to-all | bytes 2097152 | tf_op jit(solution)/shard_map/all_to_all | solution.py:76
  73.8 0.1 copy.57
  73.9 1.1 copy.58
  75.0 3.5 %all-to-all-start.2 = ((bf16[2,4,256,256]{3,2,0,1:T(8,128)(2,1)}), bf16[2,4,256,256]{3,2,0,1:T(8,128)(2,1)S(1)}, u32[]{:S(2)}, u32[]{:S(2)}) async-start(bf16[2,4,256,256]{3,2,0,1:T(8,128)(2,1)} %copy.58), calls=%async_computation.2 | async-start | bytes 2097152 | tf_op jit(solution)/shard_map/all_to_all | solution.py:79
  78.5 0.8 slice_bitcast_fusion.7
  79.3 0.9 maximum_multiply_fusion.6
  80.1 0.7 fusion.164
  80.8 0.1 maximum_multiply_fusion.8
  80.9 12.0 %all-to-all-done.2 = bf16[2,4,256,256]{3,2,0,1:T(8,128)(2,1)S(1)} async-done(((bf16[2,4,256,256]{3,2,0,1:T(8,128)(2,1)}), bf16[2,4,256,256]{3,2,0,1:T(8,128)(2,1)S(1)}, u32[]{:S(2)}, u32[]{:S(2)}) %all-to-all-start.2) | async-done | bytes 1048608 | tf_op jit(solution)/shard_map/all_to_all | solution.py:79
  92.9 0.1 fusion.168
  93.0 0.7 convolution_convert_fusion.3
  93.8 0.2 copy-done.7
  93.9 0.1 copy-done.8
  94.1 0.7 convolution_convert_fusion.2
  95.1 0.1 maximum_bitcast_fusion
  95.2 0.1 fusion.167
  95.3 0.7 copy-done.13
  96.0 0.7 convolution_convert_fusion.1
  96.7 0.7 convolution_convert_fusion
  97.7 0.1 pad_maximum_fusion.2
  97.8 1.1 copy.65
  98.9 3.5 %all-to-all-start.3 = ((bf16[2,4,256,256]{3,2,0,1:T(8,128)(2,1)}), bf16[2,4,256,256]{3,2,0,1:T(8,128)(2,1)S(1)}, u32[]{:S(2)}, u32[]{:S(2)}) async-start(bf16[2,4,256,256]{3,2,0,1:T(8,128)(2,1)} %copy.65), calls=%async_computation.3 | async-start | bytes 2097152 | tf_op jit(solution)/shard_map/all_to_all | solution.py:88
  102.4 0.1 copy.76
  102.5 0.1 copy.75
  102.6 14.2 %all-to-all-done.3 = bf16[2,4,256,256]{3,2,0,1:T(8,128)(2,1)S(1)} async-done(((bf16[2,4,256,256]{3,2,0,1:T(8,128)(2,1)}), bf16[2,4,256,256]{3,2,0,1:T(8,128)(2,1)S(1)}, u32[]{:S(2)}, u32[]{:S(2)}) %all-to-all-start.3) | async-done | bytes 1048608 | tf_op jit(solution)/shard_map/all_to_all | solution.py:88
  116.9 0.3 fusion.136
  117.2 0.3 fusion.134
  117.5 0.3 fusion.1
  117.9 0.4 fusion.143
  118.3 38.6 %all_gather.3 = f32[2,4096]{1,0:T(2,128)S(1)} all-gather(f32[2,128]{1,0:T(2,128)S(1)} %pad_maximum_fusion.3), channel_id=1, replica_groups=mesh['sx'=8,'sy'=4] {'sx','sy'}, dimensions={1}, use_global_device_ids=true | all-gather | bytes 33792 | tf_op jit(solution)/shard_map/all_gather | solution.py:92
  156.8 0.6 copy.78
  (65 shorter events, 1.5 us)
Async XLA Ops:
  2.3 33.1 %all-to-all-start = ((bf16[2,8,128,256]{3,2,0,1:T(8,128)(2,1)}), bf16[2,8,128,256]{3,2,0,1:T(8,128)(2,1)S(1)}, u32[]{:S(2)}, u32[]{:S(2)}) async-start(bf16[2,8,128,256]{3,2,0,1:T(8,128)(2,1)} %copy.47), calls=%async_computation | async-start | bytes 2097152 | tf_op jit(solution)/shard_map/all_to_all | solution.py:67
  35.4 0.9 copy-start.23
  35.4 1.0 copy-start.24
  35.4 1.0 copy-start.25
  36.4 0.9 copy-start.5
  36.4 1.0 copy-start.6
  38.4 0.9 copy-start.11
  38.4 1.0 copy-start.12
  38.4 1.0 copy-start.22
  39.4 0.9 copy-start.3
  39.4 1.0 copy-start.4
  41.4 0.9 copy-start.10
  41.4 1.0 copy-start.21
  42.3 0.9 copy-start.1
  42.3 1.0 copy-start.2
  75.0 17.9 %all-to-all-start.2 = ((bf16[2,4,256,256]{3,2,0,1:T(8,128)(2,1)}), bf16[2,4,256,256]{3,2,0,1:T(8,128)(2,1)S(1)}, u32[]{:S(2)}, u32[]{:S(2)}) async-start(bf16[2,4,256,256]{3,2,0,1:T(8,128)(2,1)} %copy.58), calls=%async_computation.2 | async-start | bytes 2097152 | tf_op jit(solution)/shard_map/all_to_all | solution.py:79
  79.2 13.7 %copy-start.14 = (bf16[256,256]{1,0:T(8,128)(2,1)S(1)}, bf16[256,256]{1,0:T(8,128)(2,1)}, u32[]{:S(2)}) copy-start(bf16[256,256]{1,0:T(8,128)(2,1)} %get-tuple-element.96) | copy-start | bytes 393220
  79.2 13.7 %copy-start.16 = (bf16[256,256]{1,0:T(8,128)(2,1)S(1)}, bf16[256,256]{1,0:T(8,128)(2,1)}, u32[]{:S(2)}) copy-start(bf16[256,256]{1,0:T(8,128)(2,1)} %get-tuple-element.99) | copy-start | bytes 393220
  79.2 13.7 %copy-start.19 = (bf16[256,256]{1,0:T(8,128)(2,1)S(1)}, bf16[256,256]{1,0:T(8,128)(2,1)}, u32[]{:S(2)}) copy-start(bf16[256,256]{1,0:T(8,128)(2,1)} %get-tuple-element.107) | copy-start | bytes 393220
  93.0 1.0 copy-start.7
  93.0 1.0 copy-start.8
  93.0 1.0 copy-start.15
  93.0 1.1 copy-start.17
  93.0 1.1 copy-start.20
  95.0 0.9 copy-start.13
  95.1 1.0 copy-start.18
  97.8 4.6 %copy-start.9 = (f32[2,128,256]{2,1,0:T(8,128)S(1)}, f32[2,128,256]{2,1,0:T(8,128)}, u32[]{:S(2)}) copy-start(f32[2,128,256]{2,1,0:T(8,128)} %param.7) | copy-start | bytes 786436
  98.9 17.9 %all-to-all-start.3 = ((bf16[2,4,256,256]{3,2,0,1:T(8,128)(2,1)}), bf16[2,4,256,256]{3,2,0,1:T(8,128)(2,1)S(1)}, u32[]{:S(2)}, u32[]{:S(2)}) async-start(bf16[2,4,256,256]{3,2,0,1:T(8,128)(2,1)} %copy.65), calls=%async_computation.3 | async-start | bytes 2097152 | tf_op jit(solution)/shard_map/all_to_all | solution.py:88
  102.4 14.5 %copy-start = (bf16[2,128,1024]{2,1,0:T(8,128)(2,1)S(1)}, bf16[2,128,1024]{2,1,0:T(8,128)(2,1)}, u32[]{:S(2)}) copy-start(bf16[2,128,1024]{2,1,0:T(8,128)(2,1)} %param.6) | copy-start | bytes 1572868
where the time goes:
time: 158 us; the launch traced here: 157 us
  blocking collectives  67.9 us (43%)
  waiting for transfers between devices  44.3 us (28%)
  local copies, waits for them, and re-layouts  15.1 us (10%)
  starting transfers between devices  14.3 us (9%)
  matrix products  8.46 us (5%)
  other arithmetic  6.72 us (4%)
    all_gather x1, blocking collectives, local(): return lax.all_gather(closed, ('sx', 'sy'), axis=1, tiled=True)  38.6 us
    all_to_all x1, blocking collectives, local(): lax.all_to_all(grouped, 'sx', split_axis=1, concat_axis=1, tiled=True)  29.3 us
    all_to_all x1, waiting for transfers between devices, local(): lax.all_to_all(current.reshape(2, count_x, rows_dev // count_x, width), '...  18.2 us
    all_to_all x1, waiting for transfers between devices, local(): lax.all_to_all(grouped, 'sy', split_axis=1, concat_axis=1, tiled=True)  14.2 us
    all_to_all x1, waiting for transfers between devices, local(): lax.all_to_all(current.reshape(2, count_y, rows_dev // count_y, width), '...  12 us
    all_to_all x1, starting transfers between devices, local(): lax.all_to_all(current.reshape(2, count_x, rows_dev // count_x, width), '...  7.31 us
    dot_general x10, matrix products, combine(): jnp.dot(joined, matrix, preferred_element_type=jnp.float32)  7.1 us
    unnamed x59, local copies, waits for them, and re-layouts  5.51 us
  transfers between devices with their start and end apart: 3, of which 3 were waited for; matrix products, arithmetic and copies ran while one was open for 6% of the time, Pallas kernels for 0%

commit v1 on v0

--- a/solution.py
+++ b/solution.py
@@ -89,7 +89,7 @@
         2, rows_dev, width
     )
     closed = close_columns(combine_rows(closing_rows, current), closing_columns)
-    return lax.all_gather(closed, ("sx", "sy"), axis=1, tiled=True)
+    return jnp.concatenate(lax.all_gather(closed, ("sx", "sy")), axis=1)
 
 
 def solution(mesh):

time: 158 us -> 158 us (level)
  no operation moved by 1% of the time
where the time goes in v1:
time: 158 us; the launch traced here: 157 us
  blocking collectives  67.9 us (43%)
  waiting for transfers between devices  44.3 us (28%)
  local copies, waits for them, and re-layouts  15.1 us (10%)
  starting transfers between devices  14.3 us (9%)
  matrix products  8.46 us (5%)
  other arithmetic  6.72 us (4%)
    all_gather x1, blocking collectives, local(): return jnp.concatenate(lax.all_gather(closed, ('sx', 'sy')), axis=1)  38.6 us
    all_to_all x1, blocking collectives, local(): lax.all_to_all(grouped, 'sx', split_axis=1, concat_axis=1, tiled=True)  29.3 us
    all_to_all x1, waiting for transfers between devices, local(): lax.all_to_all(current.reshape(2, count_x, rows_dev // count_x, width), '...  18.2 us
    all_to_all x1, waiting for transfers between devices, local(): lax.all_to_all(grouped, 'sy', split_axis=1, concat_axis=1, tiled=True)  14.2 us
    all_to_all x1, waiting for transfers between devices, local(): lax.all_to_all(current.reshape(2, count_y, rows_dev // count_y, width), '...  12 us
    all_to_all x1, starting transfers between devices, local(): lax.all_to_all(current.reshape(2, count_x, rows_dev // count_x, width), '...  7.31 us
    dot_general x10, matrix products, combine(): jnp.dot(joined, matrix, preferred_element_type=jnp.float32)  7.1 us
    unnamed x59, local copies, waits for them, and re-layouts  5.51 us
  transfers between devices with their start and end apart: 3, of which 3 were waited for; matrix products, arithmetic and copies ran while one was open for 6% of the time, Pallas kernels for 0%

profile of v1, /device:TPU:0, one launch (start us, length us, event | category | flops | bytes accessed | tf_op | source)
XLA Modules:
  0.0 157.4 jit_solution(16221818404963816740)
XLA Ops:
  0.0 2.3 %copy.47 = bf16[2,8,128,256]{3,2,0,1:T(8,128)(2,1)} copy(bf16[2,8,128,256]{3,2,1,0:T(8,128)(2,1)} %bitcast.212) | data formatting | bytes 2097152 | tf_op jit(solution)/shard_map/reshape;squeeze | solution.py:68
  2.3 7.3 %all-to-all-start = ((bf16[2,8,128,256]{3,2,0,1:T(8,128)(2,1)}), bf16[2,8,128,256]{3,2,0,1:T(8,128)(2,1)S(1)}, u32[]{:S(2)}, u32[]{:S(2)}) async-start(bf16[2,8,128,256]{3,2,0,1:T(8,128)(2,1)} %copy.47), calls=%async_computation | async-start | bytes 2097152 | tf_op jit(solution)/shard_map/all_to_all | solution.py:67
  9.6 1.9 %slice_bitcast_fusion = (bf16[2,2,256,256]{3,2,1,0:T(8,128)(2,1)S(1)}, bf16[2,2,256,256]{3,2,1,0:T(8,128)(2,1)S(1)}, bf16[2,2,256,256]{3,2,1,0:T(8,128)(2,1)S(1)...) fusion(bf16[5,2,2,256,256]{4,3,2,1,0:T(8,128)(2,1)} %param.5), kind=kLoop, calls=%fused_computation.162 | loop fusion | bytes 5242880 | tf_op jit(solution)/shard_map/squeeze | solution.py:87
  11.5 0.7 slice_bitcast_fusion.23
  12.2 0.7 fusion.156
  13.0 0.9 maximum_multiply_fusion
  13.9 0.8 slice_bitcast_fusion.15
  14.7 0.9 maximum_multiply_fusion.2
  15.6 0.8 fusion.160
  16.3 0.9 maximum_multiply_fusion.4
  17.2 18.2 %all-to-all-done = bf16[2,8,128,256]{3,2,0,1:T(8,128)(2,1)S(1)} async-done(((bf16[2,8,128,256]{3,2,0,1:T(8,128)(2,1)}), bf16[2,8,128,256]{3,2,0,1:T(8,128)(2,1)S(1)}, u32[]{:S(2)}, u32[]{:S(2)}) %all-to-all-start) | async-done | bytes 1048608 | tf_op jit(solution)/shard_map/all_to_all | solution.py:67
  35.4 0.1 fusion.171
  35.5 0.8 copy-done.23
  36.4 0.7 convolution_convert_fusion.9
  37.2 0.2 copy-done.5
  37.4 0.1 copy-done.6
  37.5 0.7 convolution_convert_fusion.8
  38.3 0.1 maximum_maximum_fusion.1
  38.4 0.1 fusion.170
  38.6 0.7 copy-done.11
  39.4 0.7 convolution_convert_fusion.7
  40.1 0.2 copy-done.3
  40.4 0.1 copy-done.4
  40.4 0.7 convolution_convert_fusion.6
  41.4 0.1 pad_maximum_fusion
  41.5 0.1 fusion.169
  41.6 0.7 copy-done.10
  42.3 0.7 convolution_convert_fusion.5
  43.0 0.2 copy-done.1
  43.3 0.1 copy-done.2
  43.4 0.7 convolution_convert_fusion.4
  44.3 0.1 pad_maximum_fusion.1
  44.4 0.1 copy.56
  44.5 29.3 %all_to_all.20 = bf16[2,8,128,256]{3,2,0,1:T(8,128)(2,1)S(1)} all-to-all(bf16[2,8,128,256]{3,2,0,1:T(8,128)(2,1)S(1)} %copy.56), channel_id=1, replica_groups=mesh['sx'=8,'sy'=4] {'sx'}, dimensions={1} | all-to-all | bytes 2097152 | tf_op jit(solution)/shard_map/all_to_all | solution.py:76
  73.8 0.1 copy.57
  73.9 1.1 copy.58
  75.0 3.5 %all-to-all-start.2 = ((bf16[2,4,256,256]{3,2,0,1:T(8,128)(2,1)}), bf16[2,4,256,256]{3,2,0,1:T(8,128)(2,1)S(1)}, u32[]{:S(2)}, u32[]{:S(2)}) async-start(bf16[2,4,256,256]{3,2,0,1:T(8,128)(2,1)} %copy.58), calls=%async_computation.2 | async-start | bytes 2097152 | tf_op jit(solution)/shard_map/all_to_all | solution.py:79
  78.5 0.8 slice_bitcast_fusion.7
  79.3 0.9 maximum_multiply_fusion.6
  80.1 0.7 fusion.164
  80.8 0.1 maximum_multiply_fusion.8
  80.9 12.0 %all-to-all-done.2 = bf16[2,4,256,256]{3,2,0,1:T(8,128)(2,1)S(1)} async-done(((bf16[2,4,256,256]{3,2,0,1:T(8,128)(2,1)}), bf16[2,4,256,256]{3,2,0,1:T(8,128)(2,1)S(1)}, u32[]{:S(2)}, u32[]{:S(2)}) %all-to-all-start.2) | async-done | bytes 1048608 | tf_op jit(solution)/shard_map/all_to_all | solution.py:79
  92.9 0.1 fusion.168
  93.0 0.7 convolution_convert_fusion.3
  93.8 0.2 copy-done.7
  93.9 0.1 copy-done.8
  94.1 0.7 convolution_convert_fusion.2
  95.1 0.1 maximum_bitcast_fusion
  95.2 0.1 fusion.167
  95.3 0.7 copy-done.13
  96.0 0.7 convolution_convert_fusion.1
  96.7 0.7 convolution_convert_fusion
  97.7 0.1 pad_maximum_fusion.2
  97.8 1.1 copy.65
  98.9 3.5 %all-to-all-start.3 = ((bf16[2,4,256,256]{3,2,0,1:T(8,128)(2,1)}), bf16[2,4,256,256]{3,2,0,1:T(8,128)(2,1)S(1)}, u32[]{:S(2)}, u32[]{:S(2)}) async-start(bf16[2,4,256,256]{3,2,0,1:T(8,128)(2,1)} %copy.65), calls=%async_computation.3 | async-start | bytes 2097152 | tf_op jit(solution)/shard_map/all_to_all | solution.py:88
  102.4 0.1 copy.76
  102.5 0.1 copy.75
  102.6 14.2 %all-to-all-done.3 = bf16[2,4,256,256]{3,2,0,1:T(8,128)(2,1)S(1)} async-done(((bf16[2,4,256,256]{3,2,0,1:T(8,128)(2,1)}), bf16[2,4,256,256]{3,2,0,1:T(8,128)(2,1)S(1)}, u32[]{:S(2)}, u32[]{:S(2)}) %all-to-all-start.3) | async-done | bytes 1048608 | tf_op jit(solution)/shard_map/all_to_all | solution.py:88
  116.9 0.3 fusion.136
  117.2 0.3 fusion.134
  117.5 0.3 fusion.1
  117.9 0.4 fusion.143
  118.3 38.6 %all-gather.1 = f32[32,2,128]{2,1,0:T(2,128)S(1)} all-gather(f32[1,2,128]{2,1,0:T(2,128)S(1)} %maximum_bitcast_fusion.9), channel_id=2, replica_groups=mesh['sx'=8,'sy'=4] {'sx','sy'}, dimensions={0}, use_global_device_ids=true | all-gather | bytes 33792 | tf_op jit(solution)/shard_map/all_gather | solution.py:92
  156.8 0.6 copy.78
  (65 shorter events, 1.5 us)
Async XLA Ops:
  2.3 33.1 %all-to-all-start = ((bf16[2,8,128,256]{3,2,0,1:T(8,128)(2,1)}), bf16[2,8,128,256]{3,2,0,1:T(8,128)(2,1)S(1)}, u32[]{:S(2)}, u32[]{:S(2)}) async-start(bf16[2,8,128,256]{3,2,0,1:T(8,128)(2,1)} %copy.47), calls=%async_computation | async-start | bytes 2097152 | tf_op jit(solution)/shard_map/all_to_all | solution.py:67
  35.4 0.9 copy-start.23
  35.4 1.0 copy-start.24
  35.4 1.0 copy-start.25
  36.4 0.9 copy-start.5
  36.4 1.0 copy-start.6
  38.4 0.9 copy-start.11
  38.4 1.0 copy-start.12
  38.4 1.0 copy-start.22
  39.4 0.9 copy-start.3
  39.4 1.0 copy-start.4
  41.4 0.9 copy-start.10
  41.4 1.0 copy-start.21
  42.3 0.9 copy-start.1
  42.3 1.0 copy-start.2
  75.0 17.9 %all-to-all-start.2 = ((bf16[2,4,256,256]{3,2,0,1:T(8,128)(2,1)}), bf16[2,4,256,256]{3,2,0,1:T(8,128)(2,1)S(1)}, u32[]{:S(2)}, u32[]{:S(2)}) async-start(bf16[2,4,256,256]{3,2,0,1:T(8,128)(2,1)} %copy.58), calls=%async_computation.2 | async-start | bytes 2097152 | tf_op jit(solution)/shard_map/all_to_all | solution.py:79
  79.2 13.7 %copy-start.14 = (bf16[256,256]{1,0:T(8,128)(2,1)S(1)}, bf16[256,256]{1,0:T(8,128)(2,1)}, u32[]{:S(2)}) copy-start(bf16[256,256]{1,0:T(8,128)(2,1)} %get-tuple-element.96) | copy-start | bytes 393220
  79.2 13.7 %copy-start.16 = (bf16[256,256]{1,0:T(8,128)(2,1)S(1)}, bf16[256,256]{1,0:T(8,128)(2,1)}, u32[]{:S(2)}) copy-start(bf16[256,256]{1,0:T(8,128)(2,1)} %get-tuple-element.99) | copy-start | bytes 393220
  79.2 13.7 %copy-start.19 = (bf16[256,256]{1,0:T(8,128)(2,1)S(1)}, bf16[256,256]{1,0:T(8,128)(2,1)}, u32[]{:S(2)}) copy-start(bf16[256,256]{1,0:T(8,128)(2,1)} %get-tuple-element.107) | copy-start | bytes 393220
  93.0 1.0 copy-start.7
  93.0 1.0 copy-start.8
  93.0 1.0 copy-start.15
  93.0 1.1 copy-start.17
  93.0 1.1 copy-start.20
  95.0 0.9 copy-start.13
  95.1 1.0 copy-start.18
  97.8 4.6 %copy-start.9 = (f32[2,128,256]{2,1,0:T(8,128)S(1)}, f32[2,128,256]{2,1,0:T(8,128)}, u32[]{:S(2)}) copy-start(f32[2,128,256]{2,1,0:T(8,128)} %param.7) | copy-start | bytes 786436
  98.9 17.9 %all-to-all-start.3 = ((bf16[2,4,256,256]{3,2,0,1:T(8,128)(2,1)}), bf16[2,4,256,256]{3,2,0,1:T(8,128)(2,1)S(1)}, u32[]{:S(2)}, u32[]{:S(2)}) async-start(bf16[2,4,256,256]{3,2,0,1:T(8,128)(2,1)} %copy.65), calls=%async_computation.3 | async-start | bytes 2097152 | tf_op jit(solution)/shard_map/all_to_all | solution.py:88
  102.4 14.5 %copy-start = (bf16[2,128,1024]{2,1,0:T(8,128)(2,1)S(1)}, bf16[2,128,1024]{2,1,0:T(8,128)(2,1)}, u32[]{:S(2)}) copy-start(bf16[2,128,1024]{2,1,0:T(8,128)(2,1)} %param.6) | copy-start | bytes 1572868
